TPU v7x, 32 devices: a whole 2x2x4 slice. The times are simulated.
32 devices in a mesh: tm: 8 (over y, x, core), freq: 4 (over z).
Axes of the slice: x: 2, y: 2, z: 4, core: 2. Of those that a mesh axis runs over, the one named last changes fastest.
Arguments:
- sfts: float32 [384, 2, 4096], P('tm', None, 'freq'), may hold values from -40 to 40
- detector_ids: int32 [384], replicated, may hold values from 0 to 2
- intersection: float32 [3, 3], replicated, may hold values from 0.3 to 1
- lags: int32 [12], replicated, may hold values from 1 to 16, as said below
- template_ids: int32 [4096, 2], P('tm'), may hold values from 0 to 63
Outputs:
- stat: float32 [4096, 4096], P('tm', 'freq')
Inputs may be any that keep to these rules, and one draw needn't show every extreme that they name: 12 distinct lags, one of them 16.
All inputs are finite; a program needn't handle non-finite values.
Results may differ from a plain program's by a relative error of at most 0.009.
Values may be sent and summed in bfloat16 or wider, within the bound.
A program may use at most 64 MiB of HBM per device.

v0:
```python
import math

import jax
import jax.numpy as jnp
from jax import lax
from jax.sharding import PartitionSpec as P

NBIN = 4096
LAGMAX = 16
NGRID = 64
PERIOD = 283


def shifted(block, axis, distance):
    devices = range(lax.axis_size(axis))
    route = [(i - distance, i) for i in devices if i - distance in devices]
    return lax.ppermute(block, axis, route)


def block_term(
    extended, first_row, ids_padded, lag_list, intersection, amplitude_idx, phase_idx, total
):
    span = extended.shape[0] - LAGMAX
    here = jnp.arange(span, dtype=jnp.int32)
    partner = here[None, :] + lag_list[:, None]
    own_rows = extended[:span].astype(jnp.float32)
    far_rows = extended[partner].astype(jnp.float32)
    det_block = lax.dynamic_slice_in_dim(ids_padded, first_row, extended.shape[0], 0)
    det_near = det_block[:span]
    det_far = det_block[partner]
    levels = jnp.arange(intersection.shape[0], dtype=jnp.int32)
    hot_near = (det_near[:, None] == levels[None, :]).astype(jnp.float32)
    hot_far = (det_far[:, :, None] == levels[None, None, :]).astype(jnp.float32)
    weight = jnp.einsum("sa,ab,lsb->ls", hot_near, intersection, hot_far)
    inside = first_row + partner < total
    weight = jnp.where(inside, weight, jnp.float32(0.0))
    re_own = own_rows[None, :, 0]
    im_own = own_rows[None, :, 1]
    re_far = far_rows[:, :, 0]
    im_far = far_rows[:, :, 1]
    pair_re = (weight[:, :, None] * (re_own * re_far + im_own * im_far)).astype(jnp.bfloat16)
    pair_im = (weight[:, :, None] * (re_own * im_far - im_own * re_far)).astype(jnp.bfloat16)
    width = extended.shape[2]
    stacked = jnp.concatenate([pair_re.reshape(-1, width), pair_im.reshape(-1, width)], 0)
    position = first_row + jnp.arange(extended.shape[0], dtype=jnp.int32)
    orbit = 2.0 * math.pi / PERIOD * (position % PERIOD).astype(jnp.float32)
    offset = 2.0 * math.pi / NGRID * phase_idx.astype(jnp.float32)
    sine = jnp.sin(offset[:, None] + orbit[None, :])
    amplitude = 8.0 + 4.0 * amplitude_idx.astype(jnp.float32)
    phase = amplitude[:, None, None] * (sine[:, partner] - sine[:, None, :span])
    rows = phase.shape[0]
    factors = jnp.concatenate(
        [
            jnp.cos(phase).reshape(rows, -1).astype(jnp.bfloat16),
            jnp.sin(phase).reshape(rows, -1).astype(jnp.bfloat16),
        ],
        1,
    )
    return jnp.dot(factors, stacked, preferred_element_type=jnp.float32)


def shards(sfts, detector_ids, intersection, lags, template_ids):
    local_power = jnp.sum(sfts[:, 0] * sfts[:, 0] + sfts[:, 1] * sfts[:, 1], axis=1)
    power = lax.psum(local_power, "freq") / NBIN
    white = (sfts * lax.rsqrt(power + 1e-06)[:, None, None]).astype(jnp.bfloat16)
    next_rim = shifted(white[:LAGMAX], "tm", -1)
    extended = jnp.concatenate([white, next_rim], 0)
    total = detector_ids.shape[0]
    ids_padded = jnp.pad(detector_ids, (0, LAGMAX))
    scale = jnp.float32(1.0 / math.sqrt(total * lags.shape[0]))
    table = lax.all_gather(template_ids, "tm", axis=0, tiled=True)
    first_row = lax.axis_index("tm") * white.shape[0]
    sums = lax.psum_scatter(
        block_term(
            extended, first_row, ids_padded, lags, intersection, table[:, 0], table[:, 1], total
        ),
        "tm",
        scatter_dimension=0,
        tiled=True,
    )
    return sums * scale


def solution(mesh):
    in_specs = (P("tm", None, "freq"), P(), P(), P(), P("tm", None))
    out_specs = P("tm", "freq")
    return jax.shard_map(shards, mesh=mesh, in_specs=in_specs, out_specs=out_specs, check_vma=False)
```

profile of v0, /device:TPU:0, one launch (start us, length us, event | category | flops | bytes accessed | tf_op | source)
XLA Modules:
  0.0 260.6 jit_solution(2296908913018294975)
XLA Ops:
  6.5 0.0 copy-start
  6.5 0.0 reduce-scatter.2.cloned.1.call-start
  6.5 1.7 add_reduce_fusion
  8.3 13.5 %psum.7 = f32[48]{0:T(128)S(1)} all-reduce(f32[48]{0:T(128)S(1)} %add_reduce_fusion), channel_id=1, replica_groups=mesh['tm'=8,'freq'=4] {'freq'}, use_global_device_ids=true, to_apply=%region_1.0 | all-reduce | flops 48 | bytes 384 | tf_op jit(solution)/shard_map/psum | solution.py:64
  21.8 1.2 multiply_convert_fusion
  23.0 1.3 collective-permute-start
  24.3 0.3 fusion.23
  24.6 0.7 compare_select_fusion
  25.4 0.1 reshape.96
  25.4 9.9 %all_gather.3 = s32[4096,2]{0,1:T(2,128)S(1)} all-gather(s32[512,2]{0,1:T(2,128)} %param.9), channel_id=1, replica_groups=mesh['tm'=8,'freq'=4] {'tm'}, dimensions={0}, use_global_device_ids=true | all-gather | bytes 36864 | tf_op jit(solution)/shard_map/all_gather | solution.py:71
  35.4 3.4 %add_sine_fusion = f32[4096,64]{0,1:T(8,128)S(1)} fusion(f32[64]{0:T(128)S(1)} %fusion.20, f32[4096]{0:T(1024)S(1)} %bitcast.65), kind=kLoop, calls=%fused_computation.25 | loop fusion | flops 262144 | bytes 1065216 | tf_op jit(solution)/shard_map/sin | solution.py:48
  38.8 0.0 copy-start.1
  38.8 0.0 copy-start.3
  38.8 6.3 %gather_fusion = f32[576,4096]{1,0:T(8,128)} fusion(f32[4096,64]{0,1:T(8,128)S(1)} %add_sine_fusion, s32[1024]{0:T(1024)S(1)} %pad_clamp_fusion), kind=kCustom, calls=%fused_computation | custom fusion | bytes 18876672 | tf_op jit(solution)/shard_map/gather | solution.py:50
  45.2 0.0 copy-done.1
  45.2 0.0 copy-done.3
  45.2 0.1 pad_dynamic-slice_fusion
  45.2 0.0 slice-start
  45.2 3.8 %gather_fusion.1 = s32[576]{0:T(1024)S(1)} fusion(s32[64]{0:T(128)S(1)} %pad_dynamic-slice_fusion, s32[1024]{0:T(1024)S(1)} %pad_clamp_fusion), kind=kCustom, calls=%fused_computation.1 | custom fusion | bytes 6912 | tf_op jit(solution)/shard_map/gather | solution.py:30
  49.0 0.1 reshape.103
  49.1 0.0 copy-done
  49.1 0.2 fusion.14
  49.3 0.3 select_reduce_fusion
  49.6 0.1 copy_bitcast_fusion
  49.7 0.0 slice-done
  49.7 4.9 %broadcast_subtract_fusion = f32[4096,12,48]{0,2,1:T(8,128)S(1)} fusion(f32[4096,12,48]{0,2,1:T(8,128)} %bitcast.59, f32[4096,48]{0,1:T(8,128)S(1)} %slice-done), kind=kLoop, calls=%fused_computation.10 | loop fusion | flops 2359296 | bytes 19660800 | tf_op jit(solution)/shard_map/sub | solution.py:50
  54.6 0.0 copy-start.2
  54.7 36.4 %cosine_convert_fusion = (bf16[4096,576]{0,1:T(8,128)(2,1)}, bf16[4096,576]{0,1:T(8,128)(2,1)}) fusion(f32[4096,12,48]{0,2,1:T(8,128)S(1)} %broadcast_subtract_fusion, f32[4096]{0:T(1024)S(1)} %bitcast.66), kind=kLoop, calls=%fused_computation.9 | loop fusion | flops 7077888 | bytes 18890752 | tf_op jit(solution)/shard_map/convert_element_type | solution.py:54
  91.1 0.0 copy-done.2
  91.1 0.1 bitcast_select_fusion
  91.2 0.1 mul.130
  91.2 0.0 collective-permute-done
  91.2 0.3 pad_maximum_fusion
  91.6 23.3 %gather_fusion.2 = bf16[576,2,1024]{2,1,0:T(2,128)(2,1)S(1)} fusion(bf16[64,2,1024]{2,1,0:T(2,128)(2,1)S(1)} %pad_maximum_fusion, s32[1024]{0:T(1024)S(1)} %pad_clamp_fusion), kind=kCustom, calls=%fused_computation.2 | custom fusion | bytes 4720896 | tf_op jit(solution)/shard_map/gather | solution.py:27
  114.9 4.5 %fusion.22 = (f32[12,48,1,1024]{3,2,1,0:T(1,128)S(1)}, f32[12,48,1,1024]{3,2,1,0:T(1,128)S(1)}) fusion(bf16[12,48,2,1024]{3,2,1,0:T(2,128)(2,1)S(1)} %bitcast.60), kind=kLoop, calls=%fused_computation.52 | loop fusion | bytes 9437184 | tf_op jit(solution)/shard_map/slice | solution.py:39
  119.4 0.0 slice-start.1
  119.4 0.0 slice-start.3
  119.4 0.5 copy.14
  120.0 0.0 slice-start.2
  120.0 0.0 slice-start.4
  120.0 0.5 copy.16
  120.6 0.9 fusion.6
  121.4 0.2 slice-done.1
  121.6 1.3 slice-done.3
  122.9 0.2 slice-done.2
  123.0 0.2 slice-done.4
  123.2 13.8 %fusion = f32[4096,1024]{1,0:T(8,128)} fusion(bf16[4096,576]{0,1:T(8,128)(2,1)S(1)} %bitcast.64, bf16[4096,576]{0,1:T(8,128)(2,1)S(1)} %bitcast.62, bf16[576,1024]{1,0:T(8,128)(2,1)S(1)} %get-tuple-element.8, bf16[576,1024]{1,0:T(8,128)(2,1)S(1)} %get-tuple-element.7), kind=kOutput, calls=%fused_computation.3 | convolution fusion | flops 9687269376 | bytes 28573696 | tf_op jit(solution)/shard_map/dot_general | solution.py:59
  137.0 0.0 reduce-scatter.2.cloned.1.call-update
  137.0 113.4 %reduce-scatter.2.cloned.1.call-done = f32[512,1024]{1,0:T(8,128)} async-done(((f32[4096,1024]{1,0:T(8,128)}), f32[512,1024]{1,0:T(8,128)}) %reduce-scatter.2.cloned.1.call-update) | async-done | bytes 2097168 | tf_op jit(solution)/shard_map/reduce_scatter | solution.py:73
  250.4 3.3 %broadcast_multiply_fusion = f32[512,1024]{1,0:T(8,128)} fusion(f32[512,1024]{1,0:T(8,128)} %reduce-scatter.2.cloned.1.call-done), kind=kLoop, calls=%fused_computation.24 | loop fusion | flops 524288 | bytes 4194304 | tf_op jit(solution)/shard_map/mul | solution.py:81
  (7 shorter events, 0.1 us)
Async XLA Ops:
  6.5 42.6 %copy-start = (f32[3,3]{1,0:T(4,128)S(1)}, f32[3,3]{1,0:T(4,128)}, u32[]{:S(2)}) copy-start(f32[3,3]{1,0:T(4,128)} %param.7) | copy-start | bytes 112
  6.5 243.9 %reduce-scatter.2.cloned.1.call-start = ((), (), s32[]{:S(2)}) async-start(), calls=%async_computation.1 | async-start | bytes 18874368 | tf_op jit(solution)/shard_map/reduce_scatter | solution.py:73
  23.0 68.2 %collective-permute-start = (bf16[16,2,1024]{2,1,0:T(2,128)(2,1)S(1)}, bf16[16,2,1024]{2,1,0:T(2,128)(2,1)S(1)}, u32[]{:S(2)}, u32[]{:S(2)}) collective-permute-start(bf16[16,2,1024]{2,1,0:T(2,128)(2,1)S(1)} %slice.56), channel_id=1, source_target_pairs={{4,0},{8,4},{12,8},{16,12},{20,16},{24,20},{28,24},{5,1},{9,5},{13... | collective-permute-start | bytes 196616 | tf_op jit(solution)/shard_map/ppermute | solution.py:17
  38.8 6.4 %copy-start.1 = (f32[4096,64]{0,1:T(8,128)}, f32[4096,64]{0,1:T(8,128)S(1)}, u32[]{:S(2)}) copy-start(f32[4096,64]{0,1:T(8,128)S(1)} %add_sine_fusion) | copy-start | bytes 3145732
  38.8 6.3 %copy-start.3 = (s32[384]{0:T(512)S(1)}, s32[384]{0:T(512)}, u32[]{:S(2)}) copy-start(s32[384]{0:T(512)} %param.6) | copy-start | bytes 4612
  45.2 4.4 %slice-start = ((f32[4096,64]{0,1:T(8,128)}), f32[4096,48]{0,1:T(8,128)S(1)}, s32[]{:S(2)}) async-start(f32[4096,64]{0,1:T(8,128)} %copy-done.1), calls=%async_computation.2 | async-start | bytes 1572864 | tf_op jit(solution)/shard_map/slice | solution.py:50
  54.6 36.4 %copy-start.2 = (s32[12]{0:T(128)S(1)}, s32[12]{0:T(128)}, u32[]{:S(2)}) copy-start(s32[12]{0:T(128)} %param.8) | copy-start | bytes 148
  119.4 2.2 slice-start.1
  119.4 3.5 %slice-start.3 = ((s8[4718592]{0:T(1024)(128)(4,1)}), s8[4194304]{0:T(1024)(128)(4,1)S(1)}, s32[]{:S(2)}) async-start(s8[4718592]{0:T(1024)(128)(4,1)} %bitcast.63), calls=%async_computation.5 | async-start | bytes 8388608
  120.0 3.1 %slice-start.2 = ((s8[4718592]{0:T(1024)(128)(4,1)}), s8[524288]{0:T(1024)(128)(4,1)S(1)}, s32[]{:S(2)}) async-start(s8[4718592]{0:T(1024)(128)(4,1)} %bitcast.61), calls=%async_computation.4 | async-start | bytes 1048576
  120.0 3.2 %slice-start.4 = ((s8[4718592]{0:T(1024)(128)(4,1)}), s8[524288]{0:T(1024)(128)(4,1)S(1)}, s32[]{:S(2)}) async-start(s8[4718592]{0:T(1024)(128)(4,1)} %bitcast.63), calls=%async_computation.6 | async-start | bytes 1048576
Sparse Core Ops, SparseCore 0:
  137.1 113.2 reduce-scatter.1
where the time goes:
time: 261 us
  waiting for transfers between devices  113 us (43%)
  other arithmetic  53.4 us (20%)
  local copies, waits for them, and re-layouts  41.5 us (16%)
  blocking collectives  23.4 us (9%)
  matrix products  13.9 us (5%)
  between operations  13.6 us (5%)
    reduce_scatter x1, waiting for transfers between devices, shards(): lax.psum_scatter(block_term(extended, first_row, ids_padded, lags, inters...  113 us
    convert_element_type x1, other arithmetic, block_term(): jnp.cos(phase).reshape(rows, -1).astype(jnp.bfloat16)  36.4 us
    gather x1, local copies, waits for them, and re-layouts, block_term(): far_rows = extended[partner].astype(jnp.float32)  23.3 us
    dot_general x1, matrix products, block_term(): return jnp.dot(factors, stacked, preferred_element_type=jnp.float32)  13.8 us
    psum x1, blocking collectives, shards(): power = lax.psum(local_power, 'freq') / NBIN  13.5 us
    all_gather x1, blocking collectives, shards(): table = lax.all_gather(template_ids, 'tm', axis=0, tiled=True)  9.9 us
    gather x1, local copies, waits for them, and re-layouts, block_term(): phase = amplitude[:, None, None] * (sine[:, partner] - sine[:, None, :span])  6.33 us
  transfers between devices with their start and end apart: 2, of which 1 were waited for; matrix products, arithmetic and copies ran while one was open for 22% of the time, Pallas kernels for 0%

commit v1 on v0

v1 whole, which is shorter than its diff:
```python
import functools
import math

import jax
import jax.numpy as jnp
import numpy as np
from jax import lax
from jax.experimental import pallas as pl
from jax.experimental.pallas import tpu as pltpu
from jax.sharding import PartitionSpec as P

NBIN = 4096
LAGMAX = 16
NGRID = 64
PERIOD = 283
PIECE = 256
CHUNK = 96
MESH = pl.DeviceIdType.MESH


def even_series(function, degree):
    nodes = np.cos(np.pi * (np.arange(64) + 0.5) / 64) * 0.125 + 0.125
    fit = np.polynomial.chebyshev.Chebyshev.fit(nodes, function(np.sqrt(nodes)), degree, domain=[0, 0.25])
    return [float(c) for c in fit.convert(kind=np.polynomial.Polynomial).coef]


SIN_SERIES = even_series(lambda y: np.sin(2 * np.pi * y) / y, 6)
COS_SERIES = even_series(lambda y: np.cos(2 * np.pi * y), 7)


def horner(series, z):
    value = jnp.full_like(z, series[-1])
    for coefficient in series[-2::-1]:
        value = value * z + coefficient
    return value


def turn_cos_sin(turns):
    y = turns - jnp.round(turns)
    z = y * y
    return horner(COS_SERIES, z), y * horner(SIN_SERIES, z)


def xor(index, bits):
    out = index
    bit = 1
    while bit <= bits:
        if bits & bit:
            out = out + bit - 2 * bit * ((index // bit) % 2)
        bit *= 2
    return out


def kernel(
    n, nf, scale,
    x_ref, det_ref, inter_ref, lag_ref, tid_ref, out_ref,
    buf, pbuf, rbuf, rcol, detcol, table, factors, white, pairs,
    bulk_send, bulk_recv, p_send, p_recv, r_send, r_recv,
):
    me = lax.axis_index("tm")
    mf = lax.axis_index("freq")
    span = x_ref.shape[0]
    rows = n * span
    nlag = lag_ref.shape[0]
    pieces = buf.shape[0]
    templ = tid_ref.shape[1]
    evens = [o for o in range(2, n, 2)]

    re = x_ref[:, 0, :]
    im = x_ref[:, 1, :]
    for p in range(pieces):
        cols = slice(p * PIECE, (p + 1) * PIECE)
        buf[p, me, 0] = re[:, cols].astype(jnp.bfloat16)
        buf[p, me, 1] = im[:, cols].astype(jnp.bfloat16)
    local = jnp.sum(re * re + im * im, axis=1, keepdims=True)
    eye = lax.broadcasted_iota(jnp.int32, (span, 128), 0) == lax.broadcasted_iota(jnp.int32, (span, 128), 1)
    local_row = jnp.sum(jnp.where(eye, local, 0.0), axis=0, keepdims=True)
    pbuf[0] = jnp.broadcast_to(local_row, (8, 128))

    barrier = pltpu.get_barrier_semaphore()
    for d in range(1, nf):
        pl.semaphore_signal(barrier, inc=1, device_id=(me, (mf + d) % nf), device_id_type=MESH)
    for o in range(1, n):
        pl.semaphore_signal(barrier, inc=1, device_id=(xor(me, o), mf), device_id_type=MESH)
    pl.semaphore_wait(barrier, nf - 1 + n - 1)

    def power_copy(d):
        return pltpu.make_async_remote_copy(
            src_ref=pbuf.at[0], dst_ref=pbuf.at[d], send_sem=p_send.at[d], recv_sem=p_recv.at[d],
            device_id=(me, (mf + d) % nf), device_id_type=MESH)

    def rate_copy(o):
        return pltpu.make_async_remote_copy(
            src_ref=rbuf.at[me], dst_ref=rbuf.at[me], send_sem=r_send.at[o], recv_sem=r_recv.at[o],
            device_id=(xor(me, o), mf), device_id_type=MESH)

    def own_copy(p, o):
        return pltpu.make_async_remote_copy(
            src_ref=buf.at[p, me], dst_ref=buf.at[p, me], send_sem=bulk_send.at[p, o], recv_sem=bulk_recv.at[p, o],
            device_id=(xor(me, o), mf), device_id_type=MESH)

    def pass_copy(p, o):
        block = xor(me, o)
        return pltpu.make_async_remote_copy(
            src_ref=buf.at[p, block], dst_ref=buf.at[p, block],
            send_sem=bulk_send.at[p, o + 1], recv_sem=bulk_recv.at[p, o + 1],
            device_id=(xor(me, 1), mf), device_id_type=MESH)

    def landed(p, o):
        block = xor(me, o)
        pltpu.make_async_remote_copy(
            src_ref=buf.at[p, block], dst_ref=buf.at[p, block],
            send_sem=bulk_send.at[p, o], recv_sem=bulk_recv.at[p, o],
            device_id=(xor(me, o), mf), device_id_type=MESH).wait_recv()

    for d in range(1, nf):
        power_copy(d).start()
    for p in range(pieces):
        for o in evens + [1]:
            own_copy(p, o).start()

    tail = rows + LAGMAX
    index = lax.broadcasted_iota(jnp.int32, (tail, 128), 0).astype(jnp.float32)
    position = index - PERIOD * jnp.floor((index + 0.5) * (1.0 / PERIOD))
    cos_i, sin_i = turn_cos_sin(position * (1.0 / PERIOD))
    for c in range(templ // 128):
        cols = slice(c * 128, (c + 1) * 128)
        cos_q, sin_q = turn_cos_sin(tid_ref[1:2, cols].astype(jnp.float32) * (1.0 / NGRID))
        amplitude = (8.0 + 4.0 * tid_ref[0:1, cols].astype(jnp.float32)) * (0.5 / math.pi)
        cos_t, sin_t = turn_cos_sin(amplitude * (sin_i * cos_q + cos_i * sin_q))
        table[0, c] = cos_t
        table[1, c] = sin_t

    for d in range(1, nf):
        power_copy(d).wait_recv()
    total = pbuf[0]
    for d in range(1, nf):
        total = total + pbuf[d]
    rbuf[me] = lax.rsqrt(total * (1.0 / NBIN) + 1e-06)

    square = lax.broadcasted_iota(jnp.int32, (128, 128), 0) == lax.broadcasted_iota(jnp.int32, (128, 128), 1)
    for c in range(rows // 128):
        ids = det_ref[0:1, c * 128:(c + 1) * 128].astype(jnp.float32)
        column = jnp.sum(jnp.where(square, ids, 0.0), axis=1, keepdims=True)
        detcol[c * 128:(c + 1) * 128, :] = jnp.broadcast_to(column, (128, 128))
    detcol[rows:tail, :] = jnp.full((LAGMAX, 128), -1.0, jnp.float32)
    white[:, :, rows:tail, :] = jnp.zeros((2, PIECE // 128, LAGMAX, 128), jnp.float32)

    for o in range(1, n):
        rate_copy(o).start()

    ndet = inter_ref.shape[0]
    block = 128

    def factor_step(l, carry):
        lag = lag_ref[l]
        for r in range(rows // block):
            here = slice(r * block, (r + 1) * block)
            there = pl.ds(r * block + lag, block)
            near = detcol[here, :]
            far = detcol[there, :]
            weight = jnp.zeros((block, 128), jnp.float32)
            for b in range(ndet):
                gain = jnp.zeros((block, 128), jnp.float32)
                for a in range(ndet):
                    gain = jnp.where(near == a, inter_ref[a, b], gain)
                weight = jnp.where(far == b, gain, weight)
            for c in range(templ // 128):
                cols = slice(c * 128, (c + 1) * 128)
                ci = table[0, c, here, :] * weight
                si = table[1, c, here, :] * weight
                cj = table[0, c, there, :]
                sj = table[1, c, there, :]
                cosine = (ci * cj + si * sj).T.astype(jnp.bfloat16)
                sine = (ci * sj - si * cj).T.astype(jnp.bfloat16)
                start = pl.multiple_of(2 * rows * l + r * block, 128)
                factors[cols, pl.ds(start, block)] = cosine
                factors[cols, pl.ds(start + rows, block)] = sine
        return carry

    def forward(p):
        for o in evens:
            landed(p, o)
            pass_copy(p, o).start()

    half = nlag // 2
    lax.fori_loop(0, half, factor_step, 0)
    forward(0)
    lax.fori_loop(half, nlag, factor_step, 0)

    for o in range(1, n):
        rate_copy_in = pltpu.make_async_remote_copy(
            src_ref=rbuf.at[xor(me, o)], dst_ref=rbuf.at[xor(me, o)], send_sem=r_send.at[o], recv_sem=r_recv.at[o],
            device_id=(xor(me, o), mf), device_id_type=MESH)
        rate_copy_in.wait_recv()
    for g in range(n):
        column = jnp.sum(jnp.where(eye, rbuf[g, 0:1, :], 0.0), axis=1, keepdims=True)
        rcol[g * span:(g + 1) * span, :] = jnp.broadcast_to(column, (span, 128))

    def piece_step(p, carry):
        for o in range(1, n, 2):
            landed(p, o)

        @pl.when(p + 1 < pieces)
        def _():
            forward(p + 1)

        for g in range(n):
            here = slice(g * span, (g + 1) * span)
            rate = rcol[here, :]
            for c in range(2):
                for h in range(PIECE // 128):
                    white[c, h, here, :] = buf[p, g, c, :, h * 128:(h + 1) * 128].astype(jnp.float32) * rate

        def pair_step(l, inner):
            lag = lag_ref[l]
            for r in range(rows // CHUNK):
                here = slice(r * CHUNK, (r + 1) * CHUNK)
                there = pl.ds(r * CHUNK + lag, CHUNK)
                start = pl.multiple_of(2 * rows * l + r * CHUNK, 32)
                for h in range(PIECE // 128):
                    cols = slice(h * 128, (h + 1) * 128)
                    a = white[0, h, here, :]
                    b = white[1, h, here, :]
                    c = white[0, h, there, :]
                    d = white[1, h, there, :]
                    pairs[pl.ds(start, CHUNK), cols] = (a * c + b * d).astype(jnp.bfloat16)
                    pairs[pl.ds(start + rows, CHUNK), cols] = (a * d - b * c).astype(jnp.bfloat16)
            return inner

        lax.fori_loop(0, nlag, pair_step, 0)
        product = jnp.dot(factors[...], pairs[...], preferred_element_type=jnp.float32)
        out_ref[:, pl.ds(pl.multiple_of(p * PIECE, PIECE), PIECE)] = product * scale
        return carry

    lax.fori_loop(0, pieces, piece_step, 0)

    for d in range(1, nf):
        power_copy(d).wait_send()
    for o in range(1, n):
        rate_copy(o).wait_send()

    def drain(p, carry):
        for o in evens + [1]:
            own_copy(p, o).wait_send()
        for o in evens:
            pass_copy(p, o).wait_send()
        return carry

    lax.fori_loop(0, pieces, drain, 0)


def shards(n, nf, sfts, detector_ids, intersection, lags, template_ids):
    span, _, width = sfts.shape
    rows = detector_ids.shape[0]
    nlag = lags.shape[0]
    templ = template_ids.shape[0]
    pieces = width // PIECE
    vmem = pl.BlockSpec(memory_space=pltpu.VMEM)
    smem = pl.BlockSpec(memory_space=pltpu.SMEM)
    scale = 1.0 / math.sqrt(rows * nlag)
    return pl.pallas_call(
        functools.partial(kernel, n, nf, scale),
        out_shape=jax.ShapeDtypeStruct((templ, width), jnp.float32),
        in_specs=[vmem, vmem, smem, smem, vmem],
        out_specs=vmem,
        scratch_shapes=[
            pltpu.VMEM((pieces, n, 2, span, PIECE), jnp.bfloat16),
            pltpu.VMEM((nf, 8, 128), jnp.float32),
            pltpu.VMEM((n, 8, 128), jnp.float32),
            pltpu.VMEM((rows, 128), jnp.float32),
            pltpu.VMEM((rows + LAGMAX, 128), jnp.float32),
            pltpu.VMEM((2, templ // 128, rows + LAGMAX, 128), jnp.float32),
            pltpu.VMEM((templ, 2 * rows * nlag), jnp.bfloat16),
            pltpu.VMEM((2, PIECE // 128, rows + LAGMAX, 128), jnp.float32),
            pltpu.VMEM((2 * rows * nlag, PIECE), jnp.bfloat16),
            pltpu.SemaphoreType.DMA((pieces, n)),
            pltpu.SemaphoreType.DMA((pieces, n)),
            pltpu.SemaphoreType.DMA((nf,)),
            pltpu.SemaphoreType.DMA((nf,)),
            pltpu.SemaphoreType.DMA((n,)),
            pltpu.SemaphoreType.DMA((n,)),
        ],
        compiler_params=pltpu.CompilerParams(
            collective_id=0, has_side_effects=True, vmem_limit_bytes=60 * 1024 * 1024
        ),
    )(sfts, detector_ids.reshape(1, rows), intersection, lags, template_ids.T)


def solution(mesh):
    n, nf = mesh.shape["tm"], mesh.shape["freq"]
    in_specs = (P("tm", None, "freq"), P(), P(), P(), P("tm", None))
    return jax.shard_map(
        functools.partial(shards, n, nf), mesh=mesh, in_specs=in_specs, out_specs=P("tm", "freq"), check_vma=False
    )
```

time: 261 us -> 43.4 us (0.17)
  waiting for transfers between devices: 113 us -> 0 us
  other arithmetic: 53.4 us -> 0 us
  Pallas kernels: 0 us -> 38.8 us
  local copies, waits for them, and re-layouts: 41.5 us -> 4.4 us
  blocking collectives: 23.4 us -> 0 us
  matrix products: 13.9 us -> 0 us
  between operations: 13.6 us -> 0.01 us
    reduce_scatter x1 -> x0, waiting for transfers between devices: 113 us -> none  [shards(): lax.psum_scatter(block_term(extended, first_row, ids_padded, lags, inters...]
    pallas_call x0 -> x1, Pallas kernels: none -> 38.8 us  [shards(): pl.pallas_call(functools.partial(kernel, n, nf, scale), out_shape=jax.Sha...]
    convert_element_type x3 -> x0, other arithmetic: 38.5 us -> none  [the longest x1 36.4 us: block_term(): jnp.cos(phase).reshape(rows, -1).astype(jnp.bfloat16)]
    gather x4 -> x0, local copies, waits for them, and re-layouts: 33.5 us -> none  [the longest x1 23.3 us: block_term(): far_rows = extended[partner].astype(jnp.float32)]
    dot_general x1 -> x0, matrix products: 13.8 us -> none  [block_term(): return jnp.dot(factors, stacked, preferred_element_type=jnp.float32)]
    psum x1 -> x0, blocking collectives: 13.5 us -> none  [shards(): power = lax.psum(local_power, 'freq') / NBIN]
    all_gather x1 -> x0, blocking collectives: 9.9 us -> none  [shards(): table = lax.all_gather(template_ids, 'tm', axis=0, tiled=True)]
    sub x1 -> x0, other arithmetic: 4.94 us -> none  [block_term(): phase = amplitude[:, None, None] * (sine[:, partner] - sine[:, None, :span])]
  transfers between devices with their start and end apart: 2 -> 0, of which waited for: 1 -> 0; matrix products, arithmetic and copies ran while one was open for 22% -> 0% of each run, Pallas kernels for 0% -> 0%
where the time goes in v1:
time: 43.4 us; the launch traced here: 43.3 us
  Pallas kernels  38.8 us (89%)
  local copies, waits for them, and re-layouts  4.4 us (10%)
    pallas_call x1, Pallas kernels, shards(): pl.pallas_call(functools.partial(kernel, n, nf, scale), out_shape=jax.Sha...  38.8 us
    unnamed x1, local copies, waits for them, and re-layouts  3.16 us
    reshape x1, local copies, waits for them, and re-layouts, shards(): detector_ids.reshape(1, rows)  1.24 us

profile of v1, /device:TPU:0, one launch (start us, length us, event | category | flops | bytes accessed | tf_op | source)
XLA Modules:
  0.0 43.3 jit_solution(4523997058088704460)
XLA Ops:
  0.0 1.2 %reshape.3.det_ref = s32[1,384]{1,0:T(1,128)} reshape(s32[384]{0:T(512)} %param.6) | data formatting | bytes 3072 | tf_op jit(solution)/shard_map/reshape | solution.py:287
  1.2 38.8 %shard_map.55 = f32[512,1024]{1,0:T(8,128)} custom-call(f32[48,2,1024]{2,1,0:T(2,128)} %x_ref.1, s32[1,384]{1,0:T(1,128)} %reshape.3.det_ref, f32[3,3]{1,0:T(4,128)} %inter_ref.1, s32[12]{0:T(128)} %lag_ref.1, s32[2,512]{1,0:T(2,128)} %bitcast.1), custom_call_target="tpu_custom_call" | custom-call | tf_op jit(solution)/shard_map/pallas_call | solution.py:262
  40.1 3.2 %copy.7 = f32[512,1024]{1,0:T(8,128)} copy(f32[512,1024]{1,0:T(8,128)} %shard_map.55) | data formatting | bytes 4194304

commit v2 on v1

--- a/solution.py
+++ b/solution.py
@@ -14,7 +14,8 @@
 NGRID = 64
 PERIOD = 283
 PIECE = 256
-CHUNK = 96
+CHUNK = 32
+GROUP = 2
 MESH = pl.DeviceIdType.MESH
 
 
@@ -54,7 +55,7 @@
 def kernel(
     n, nf, scale,
     x_ref, det_ref, inter_ref, lag_ref, tid_ref, out_ref,
-    buf, pbuf, rbuf, rcol, detcol, table, factors, white, pairs,
+    buf, pbuf, rbuf, rcol, detcol, weights, table, turned, factors, white, pairs_a, pairs_b, acc,
     bulk_send, bulk_recv, p_send, p_recv, r_send, r_recv,
 ):
     me = lax.axis_index("tm")
@@ -64,6 +65,11 @@
     nlag = lag_ref.shape[0]
     pieces = buf.shape[0]
     templ = tid_ref.shape[1]
+    kept = weights.shape[2]
+    terms = weights.shape[1]
+    tail = detcol.shape[0]
+    groups = nlag // GROUP
+    depth = 2 * kept * GROUP
     evens = [o for o in range(2, n, 2)]
 
     re = x_ref[:, 0, :]
@@ -119,8 +125,7 @@
         for o in evens + [1]:
             own_copy(p, o).start()
 
-    tail = rows + LAGMAX
-    index = lax.broadcasted_iota(jnp.int32, (tail, 128), 0).astype(jnp.float32)
+    index = lax.broadcasted_iota(jnp.int32, (kept + LAGMAX, 128), 0).astype(jnp.float32)
     position = index - PERIOD * jnp.floor((index + 0.5) * (1.0 / PERIOD))
     cos_i, sin_i = turn_cos_sin(position * (1.0 / PERIOD))
     for c in range(templ // 128):
@@ -131,51 +136,44 @@
         table[0, c] = cos_t
         table[1, c] = sin_t
 
-    for d in range(1, nf):
-        power_copy(d).wait_recv()
-    total = pbuf[0]
-    for d in range(1, nf):
-        total = total + pbuf[d]
-    rbuf[me] = lax.rsqrt(total * (1.0 / NBIN) + 1e-06)
-
     square = lax.broadcasted_iota(jnp.int32, (128, 128), 0) == lax.broadcasted_iota(jnp.int32, (128, 128), 1)
     for c in range(rows // 128):
-        ids = det_ref[0:1, c * 128:(c + 1) * 128].astype(jnp.float32)
+        ids = det_ref[c * 128:(c + 1) * 128].astype(jnp.float32)[None, :]
         column = jnp.sum(jnp.where(square, ids, 0.0), axis=1, keepdims=True)
         detcol[c * 128:(c + 1) * 128, :] = jnp.broadcast_to(column, (128, 128))
-    detcol[rows:tail, :] = jnp.full((LAGMAX, 128), -1.0, jnp.float32)
-    white[:, :, rows:tail, :] = jnp.zeros((2, PIECE // 128, LAGMAX, 128), jnp.float32)
-
-    for o in range(1, n):
-        rate_copy(o).start()
+    detcol[rows:tail, :] = jnp.full((tail - rows, 128), -1.0, jnp.float32)
+    white[:, :, rows:tail, :] = jnp.zeros((2, PIECE // 128, tail - rows, 128), jnp.float32)
 
     ndet = inter_ref.shape[0]
-    block = 128
-
-    def factor_step(l, carry):
+    level = lax.broadcasted_iota(jnp.int32, (kept, 128), 0) < PERIOD
+
+    def weight_step(l, carry):
         lag = lag_ref[l]
-        for r in range(rows // block):
-            here = slice(r * block, (r + 1) * block)
-            there = pl.ds(r * block + lag, block)
-            near = detcol[here, :]
-            far = detcol[there, :]
-            weight = jnp.zeros((block, 128), jnp.float32)
+        for m in range(terms):
+            near = detcol[m * PERIOD:m * PERIOD + kept, :]
+            far = detcol[pl.ds(m * PERIOD + lag, kept), :]
+            weight = jnp.zeros((kept, 128), jnp.float32)
             for b in range(ndet):
-                gain = jnp.zeros((block, 128), jnp.float32)
+                gain = jnp.zeros((kept, 128), jnp.float32)
                 for a in range(ndet):
                     gain = jnp.where(near == a, inter_ref[a, b], gain)
                 weight = jnp.where(far == b, gain, weight)
+            weights[l, m] = jnp.where(level, weight, 0.0)
+        return carry
+
+    def factor_step(g, carry):
+        for k in range(GROUP):
+            lag = lag_ref[g * GROUP + k]
             for c in range(templ // 128):
                 cols = slice(c * 128, (c + 1) * 128)
-                ci = table[0, c, here, :] * weight
-                si = table[1, c, here, :] * weight
-                cj = table[0, c, there, :]
-                sj = table[1, c, there, :]
-                cosine = (ci * cj + si * sj).T.astype(jnp.bfloat16)
-                sine = (ci * sj - si * cj).T.astype(jnp.bfloat16)
-                start = pl.multiple_of(2 * rows * l + r * block, 128)
-                factors[cols, pl.ds(start, block)] = cosine
-                factors[cols, pl.ds(start + rows, block)] = sine
+                ci = table[0, c, 0:kept, :]
+                si = table[1, c, 0:kept, :]
+                cj = table[0, c, pl.ds(lag, kept), :]
+                sj = table[1, c, pl.ds(lag, kept), :]
+                turned[2 * k * kept:(2 * k + 1) * kept, cols] = (ci * cj + si * sj).astype(jnp.bfloat16)
+                turned[(2 * k + 1) * kept:(2 * k + 2) * kept, cols] = (ci * sj - si * cj).astype(jnp.bfloat16)
+        for b in range(depth // 128):
+            factors[g, :, b * 128:(b + 1) * 128] = turned[b * 128:(b + 1) * 128, :].T
         return carry
 
     def forward(p):
@@ -183,10 +181,24 @@
             landed(p, o)
             pass_copy(p, o).start()
 
-    half = nlag // 2
-    lax.fori_loop(0, half, factor_step, 0)
+    first = groups // 3
+    second = 2 * groups // 3
+    lax.fori_loop(0, first, factor_step, 0)
+    for d in range(1, nf):
+        power_copy(d).wait_recv()
+    total = pbuf[0]
+    for d in range(1, nf):
+        total = total + pbuf[d]
+    rbuf[me] = lax.rsqrt(total * (1.0 / NBIN) + 1e-06)
+
+    for o in range(1, n):
+        rate_copy(o).start()
+
     forward(0)
-    lax.fori_loop(half, nlag, factor_step, 0)
+    lax.fori_loop(first, second, factor_step, 0)
+    forward(1)
+    lax.fori_loop(second, groups, factor_step, 0)
+    lax.fori_loop(0, nlag, weight_step, 0)
 
     for o in range(1, n):
         rate_copy_in = pltpu.make_async_remote_copy(
@@ -201,9 +213,9 @@
         for o in range(1, n, 2):
             landed(p, o)
 
-        @pl.when(p + 1 < pieces)
+        @pl.when(p + 2 < pieces)
         def _():
-            forward(p + 1)
+            forward(p + 2)
 
         for g in range(n):
             here = slice(g * span, (g + 1) * span)
@@ -212,25 +224,45 @@
                 for h in range(PIECE // 128):
                     white[c, h, here, :] = buf[p, g, c, :, h * 128:(h + 1) * 128].astype(jnp.float32) * rate
 
-        def pair_step(l, inner):
-            lag = lag_ref[l]
-            for r in range(rows // CHUNK):
-                here = slice(r * CHUNK, (r + 1) * CHUNK)
-                there = pl.ds(r * CHUNK + lag, CHUNK)
-                start = pl.multiple_of(2 * rows * l + r * CHUNK, 32)
-                for h in range(PIECE // 128):
-                    cols = slice(h * 128, (h + 1) * 128)
-                    a = white[0, h, here, :]
-                    b = white[1, h, here, :]
-                    c = white[0, h, there, :]
-                    d = white[1, h, there, :]
-                    pairs[pl.ds(start, CHUNK), cols] = (a * c + b * d).astype(jnp.bfloat16)
-                    pairs[pl.ds(start + rows, CHUNK), cols] = (a * d - b * c).astype(jnp.bfloat16)
-            return inner
-
-        lax.fori_loop(0, nlag, pair_step, 0)
-        product = jnp.dot(factors[...], pairs[...], preferred_element_type=jnp.float32)
-        out_ref[:, pl.ds(pl.multiple_of(p * PIECE, PIECE), PIECE)] = product * scale
+        def make_pairs(g, pairs):
+            for r in range(0, kept, CHUNK):
+                for k in range(GROUP):
+                    l = g * GROUP + k
+                    lag = lag_ref[l]
+                    for h in range(PIECE // 128):
+                        cols = slice(h * 128, (h + 1) * 128)
+                        real = None
+                        for m in range(terms):
+                            if m * PERIOD + r >= rows:
+                                continue
+                            here = slice(m * PERIOD + r, m * PERIOD + r + CHUNK)
+                            there = pl.ds(m * PERIOD + r + lag, CHUNK)
+                            w = weights[l, m, r:r + CHUNK, :]
+                            a = white[0, h, here, :]
+                            b = white[1, h, here, :]
+                            c = white[0, h, there, :]
+                            d = white[1, h, there, :]
+                            re_m = w * (a * c + b * d)
+                            im_m = w * (a * d - b * c)
+                            real = re_m if m == 0 else real + re_m
+                            imag = im_m if m == 0 else imag + im_m
+                        start = 2 * k * kept + r
+                        pairs[start:start + CHUNK, cols] = real.astype(jnp.bfloat16)
+                        pairs[start + kept:start + kept + CHUNK, cols] = imag.astype(jnp.bfloat16)
+
+        slots = (pairs_a, pairs_b)
+        make_pairs(0, slots[0])
+        for g in range(groups):
+            if g + 1 < groups:
+                make_pairs(g + 1, slots[(g + 1) % 2])
+            product = jnp.dot(factors[g], slots[g % 2][...], preferred_element_type=jnp.float32)
+            if g == 0:
+                acc[...] = product
+            elif g + 1 < groups:
+                acc[...] += product
+            else:
+                cols = pl.ds(pl.multiple_of(p * PIECE, PIECE), PIECE)
+                out_ref[:, cols] = ((acc[...] + product) * scale).astype(out_ref.dtype)
         return carry
 
     lax.fori_loop(0, pieces, piece_step, 0)
@@ -256,12 +288,17 @@
     nlag = lags.shape[0]
     templ = template_ids.shape[0]
     pieces = width // PIECE
+    kept = -(-PERIOD // CHUNK) * CHUNK
+    terms = -(-rows // PERIOD)
+    tail = (terms - 1) * PERIOD + kept + LAGMAX
+    tail = -(-tail // 8) * 8
+    depth = 2 * kept * GROUP
     vmem = pl.BlockSpec(memory_space=pltpu.VMEM)
     smem = pl.BlockSpec(memory_space=pltpu.SMEM)
     scale = 1.0 / math.sqrt(rows * nlag)
-    return pl.pallas_call(
+    stat = pl.pallas_call(
         functools.partial(kernel, n, nf, scale),
-        out_shape=jax.ShapeDtypeStruct((templ, width), jnp.float32),
+        out_shape=jax.ShapeDtypeStruct((templ, width), jnp.bfloat16),
         in_specs=[vmem, vmem, smem, smem, vmem],
         out_specs=vmem,
         scratch_shapes=[
@@ -269,11 +306,15 @@
             pltpu.VMEM((nf, 8, 128), jnp.float32),
             pltpu.VMEM((n, 8, 128), jnp.float32),
             pltpu.VMEM((rows, 128), jnp.float32),
-            pltpu.VMEM((rows + LAGMAX, 128), jnp.float32),
-            pltpu.VMEM((2, templ // 128, rows + LAGMAX, 128), jnp.float32),
-            pltpu.VMEM((templ, 2 * rows * nlag), jnp.bfloat16),
-            pltpu.VMEM((2, PIECE // 128, rows + LAGMAX, 128), jnp.float32),
-            pltpu.VMEM((2 * rows * nlag, PIECE), jnp.bfloat16),
+            pltpu.VMEM((tail, 128), jnp.float32),
+            pltpu.VMEM((nlag, terms, kept, 128), jnp.float32),
+            pltpu.VMEM((2, templ // 128, kept + LAGMAX, 128), jnp.float32),
+            pltpu.VMEM((depth, templ), jnp.bfloat16),
+            pltpu.VMEM((nlag // GROUP, templ, depth), jnp.bfloat16),
+            pltpu.VMEM((2, PIECE // 128, tail, 128), jnp.float32),
+            pltpu.VMEM((depth, PIECE), jnp.bfloat16),
+            pltpu.VMEM((depth, PIECE), jnp.bfloat16),
+            pltpu.VMEM((templ, PIECE), jnp.float32),
             pltpu.SemaphoreType.DMA((pieces, n)),
             pltpu.SemaphoreType.DMA((pieces, n)),
             pltpu.SemaphoreType.DMA((nf,)),
@@ -282,9 +323,10 @@
             pltpu.SemaphoreType.DMA((n,)),
         ],
         compiler_params=pltpu.CompilerParams(
-            collective_id=0, has_side_effects=True, vmem_limit_bytes=60 * 1024 * 1024
+            collective_id=0, has_side_effects=True, vmem_limit_bytes=36 * 1024 * 1024
         ),
-    )(sfts, detector_ids.reshape(1, rows), intersection, lags, template_ids.T)
+    )(sfts, detector_ids, intersection, lags, template_ids.T)
+    return stat.astype(jnp.float32)
 
 
 def solution(mesh):

time: 43.4 us -> 44.5 us (1.025)
  other arithmetic: 0 us -> 1.57 us
  local copies, waits for them, and re-layouts: 4.4 us -> 3.7 us
    convert_element_type x0 -> x1, other arithmetic: none -> 1.57 us  [shards(): return stat.astype(jnp.float32)]
    reshape x1 -> x0, local copies, waits for them, and re-layouts: 1.24 us -> none  [shards(): detector_ids.reshape(1, rows)]
    unnamed x1 -> x10, local copies, waits for them, and re-layouts: 3.16 us -> 3.7 us
where the time goes in v2:
time: 44.5 us
  Pallas kernels  39.2 us (88%)
  local copies, waits for them, and re-layouts  3.7 us (8%)
  other arithmetic  1.57 us (4%)
    pallas_call x1, Pallas kernels, shards(): pl.pallas_call(functools.partial(kernel, n, nf, scale), out_shape=jax.Sha...  39.2 us
    unnamed x10, local copies, waits for them, and re-layouts  3.7 us
    convert_element_type x1, other arithmetic, shards(): return stat.astype(jnp.float32)  1.57 us

profile of v2, /device:TPU:0, one launch (start us, length us, event | category | flops | bytes accessed | tf_op | source)
XLA Modules:
  0.0 44.5 jit_solution(14725108612741427625)
XLA Ops:
  0.0 0.0 copy-start
  0.0 1.0 %copy-done = f32[48,2,1024]{2,1,0:T(2,128)S(1)} copy-done((f32[48,2,1024]{2,1,0:T(2,128)S(1)}, f32[48,2,1024]{2,1,0:T(2,128)}, u32[]{:S(2)}) %copy-start) | copy-done | bytes 393240
  1.0 0.0 copy-start.1
  1.0 0.7 %copy-done.1 = s32[512,2]{0,1:T(2,128)S(1)} copy-done((s32[512,2]{0,1:T(2,128)S(1)}, s32[512,2]{0,1:T(2,128)}, u32[]{:S(2)}) %copy-start.1) | copy-done | bytes 4120
  1.7 0.0 copy-start.2
  1.7 0.7 %copy-done.2 = s32[384]{0:T(512)S(1)} copy-done((s32[384]{0:T(512)S(1)}, s32[384]{0:T(512)}, u32[]{:S(2)}) %copy-start.2) | copy-done | bytes 1560
  2.4 0.0 copy-start.3
  2.4 0.7 %copy-done.3 = f32[3,3]{1,0:T(4,128)S(1)} copy-done((f32[3,3]{1,0:T(4,128)S(1)}, f32[3,3]{1,0:T(4,128)}, u32[]{:S(2)}) %copy-start.3) | copy-done | bytes 60
  3.0 0.0 copy-start.4
  3.1 0.7 %copy-done.4 = s32[12]{0:T(128)S(1)} copy-done((s32[12]{0:T(128)S(1)}, s32[12]{0:T(128)}, u32[]{:S(2)}) %copy-start.4) | copy-done | bytes 72
  3.7 39.2 %shard_map.55 = bf16[512,1024]{1,0:T(8,128)(2,1)S(1)} custom-call(f32[48,2,1024]{2,1,0:T(2,128)S(1)} %copy-done, s32[384]{0:T(512)S(1)} %copy-done.2, f32[3,3]{1,0:T(4,128)S(1)} %copy-done.3, s32[12]{0:T(128)S(1)} %copy-done.4, s32[2,512]{1,0:T(2,128)S(1)} %bitcast.1), custom_call_target="tpu_custom_call" | custom-call | tf_op jit(solution)/shard_map/pallas_call | solution.py:299
  43.0 1.6 %convert_element_type.3 = f32[512,1024]{1,0:T(8,128)} convert(bf16[512,1024]{1,0:T(8,128)(2,1)S(1)} %shard_map.55) | non-fusion elementwise | flops 524288 | bytes 3145728 | tf_op jit(solution)/shard_map/convert_element_type | solution.py:329
Async XLA Ops:
  0.0 1.0 %copy-start = (f32[48,2,1024]{2,1,0:T(2,128)S(1)}, f32[48,2,1024]{2,1,0:T(2,128)}, u32[]{:S(2)}) copy-start(f32[48,2,1024]{2,1,0:T(2,128)} %x_ref.1) | copy-start | bytes 1179652
  1.0 0.7 %copy-start.1 = (s32[512,2]{0,1:T(2,128)S(1)}, s32[512,2]{0,1:T(2,128)}, u32[]{:S(2)}) copy-start(s32[512,2]{0,1:T(2,128)} %param.9) | copy-start | bytes 12292
  1.7 0.7 %copy-start.2 = (s32[384]{0:T(512)S(1)}, s32[384]{0:T(512)}, u32[]{:S(2)}) copy-start(s32[384]{0:T(512)} %det_ref.1) | copy-start | bytes 4612
  2.4 0.7 %copy-start.3 = (f32[3,3]{1,0:T(4,128)S(1)}, f32[3,3]{1,0:T(4,128)}, u32[]{:S(2)}) copy-start(f32[3,3]{1,0:T(4,128)} %inter_ref.1) | copy-start | bytes 112
  3.0 0.7 %copy-start.4 = (s32[12]{0:T(128)S(1)}, s32[12]{0:T(128)}, u32[]{:S(2)}) copy-start(s32[12]{0:T(128)} %lag_ref.1) | copy-start | bytes 148

commit v3 on v1

--- a/solution.py
+++ b/solution.py
@@ -131,23 +131,13 @@
         table[0, c] = cos_t
         table[1, c] = sin_t
 
-    for d in range(1, nf):
-        power_copy(d).wait_recv()
-    total = pbuf[0]
-    for d in range(1, nf):
-        total = total + pbuf[d]
-    rbuf[me] = lax.rsqrt(total * (1.0 / NBIN) + 1e-06)
-
     square = lax.broadcasted_iota(jnp.int32, (128, 128), 0) == lax.broadcasted_iota(jnp.int32, (128, 128), 1)
     for c in range(rows // 128):
-        ids = det_ref[0:1, c * 128:(c + 1) * 128].astype(jnp.float32)
+        ids = det_ref[c * 128:(c + 1) * 128].astype(jnp.float32)[None, :]
         column = jnp.sum(jnp.where(square, ids, 0.0), axis=1, keepdims=True)
         detcol[c * 128:(c + 1) * 128, :] = jnp.broadcast_to(column, (128, 128))
     detcol[rows:tail, :] = jnp.full((LAGMAX, 128), -1.0, jnp.float32)
     white[:, :, rows:tail, :] = jnp.zeros((2, PIECE // 128, LAGMAX, 128), jnp.float32)
-
-    for o in range(1, n):
-        rate_copy(o).start()
 
     ndet = inter_ref.shape[0]
     block = 128
@@ -185,6 +175,16 @@
 
     half = nlag // 2
     lax.fori_loop(0, half, factor_step, 0)
+    for d in range(1, nf):
+        power_copy(d).wait_recv()
+    total = pbuf[0]
+    for d in range(1, nf):
+        total = total + pbuf[d]
+    rbuf[me] = lax.rsqrt(total * (1.0 / NBIN) + 1e-06)
+
+    for o in range(1, n):
+        rate_copy(o).start()
+
     forward(0)
     lax.fori_loop(half, nlag, factor_step, 0)
 
@@ -230,7 +230,7 @@
 
         lax.fori_loop(0, nlag, pair_step, 0)
         product = jnp.dot(factors[...], pairs[...], preferred_element_type=jnp.float32)
-        out_ref[:, pl.ds(pl.multiple_of(p * PIECE, PIECE), PIECE)] = product * scale
+        out_ref[:, pl.ds(pl.multiple_of(p * PIECE, PIECE), PIECE)] = (product * scale).astype(out_ref.dtype)
         return carry
 
     lax.fori_loop(0, pieces, piece_step, 0)
@@ -259,9 +259,9 @@
     vmem = pl.BlockSpec(memory_space=pltpu.VMEM)
     smem = pl.BlockSpec(memory_space=pltpu.SMEM)
     scale = 1.0 / math.sqrt(rows * nlag)
-    return pl.pallas_call(
+    stat = pl.pallas_call(
         functools.partial(kernel, n, nf, scale),
-        out_shape=jax.ShapeDtypeStruct((templ, width), jnp.float32),
+        out_shape=jax.ShapeDtypeStruct((templ, width), jnp.bfloat16),
         in_specs=[vmem, vmem, smem, smem, vmem],
         out_specs=vmem,
         scratch_shapes=[
@@ -284,7 +284,8 @@
         compiler_params=pltpu.CompilerParams(
             collective_id=0, has_side_effects=True, vmem_limit_bytes=60 * 1024 * 1024
         ),
-    )(sfts, detector_ids.reshape(1, rows), intersection, lags, template_ids.T)
+    )(sfts, detector_ids, intersection, lags, template_ids.T)
+    return stat.astype(jnp.float32)
 
 
 def solution(mesh):

time: 43.4 us -> 41.3 us (0.952)
  local copies, waits for them, and re-layouts: 4.4 us -> 0 us
  other arithmetic: 0 us -> 2.79 us
    unnamed x1 -> x0, local copies, waits for them, and re-layouts: 3.16 us -> none
    convert_element_type x0 -> x1, other arithmetic: none -> 2.79 us  [shards(): return stat.astype(jnp.float32)]
    reshape x1 -> x0, local copies, waits for them, and re-layouts: 1.24 us -> none  [shards(): detector_ids.reshape(1, rows)]
    pallas_call x1, Pallas kernels: 38.8 us -> 38.4 us  [shards(): pl.pallas_call(functools.partial(kernel, n, nf, scale), out_shape=jax.Sha...]
where the time goes in v3:
time: 41.3 us; the launch traced here: 41.2 us
  Pallas kernels  38.4 us (93%)
  other arithmetic  2.79 us (7%)
    pallas_call x1, Pallas kernels, shards(): pl.pallas_call(functools.partial(kernel, n, nf, scale), out_shape=jax.Sha...  38.4 us
    convert_element_type x1, other arithmetic, shards(): return stat.astype(jnp.float32)  2.79 us

profile of v3, /device:TPU:0, one launch (start us, length us, event | category | flops | bytes accessed | tf_op | source)
XLA Modules:
  0.0 41.2 jit_solution(15047596686049634571)
XLA Ops:
  0.0 38.4 %shard_map.55 = bf16[512,1024]{1,0:T(8,128)(2,1)} custom-call(f32[48,2,1024]{2,1,0:T(2,128)} %x_ref.1, s32[384]{0:T(512)} %det_ref.1, f32[3,3]{1,0:T(4,128)} %inter_ref.1, s32[12]{0:T(128)} %lag_ref.1, s32[2,512]{1,0:T(2,128)} %bitcast.1), custom_call_target="tpu_custom_call" | custom-call | tf_op jit(solution)/shard_map/pallas_call | solution.py:262
  38.4 2.8 %convert_element_type.3 = f32[512,1024]{1,0:T(8,128)} convert(bf16[512,1024]{1,0:T(8,128)(2,1)} %shard_map.55) | non-fusion elementwise | flops 524288 | bytes 3145728 | tf_op jit(solution)/shard_map/convert_element_type | solution.py:288
